TPU v7x, 256 devices: a whole 4x4x8 slice. The times are simulated.
256 devices in a mesh: vp: 64 (over y, z, core), rep: 4 (over x).
Axes of the slice: x: 4, y: 4, z: 8, core: 2. Of those that a mesh axis runs over, the one named last changes fastest.
Arguments:
- features: bfloat16 [524288, 256], P(('vp', 'rep')), may hold values from -48 to 48
- tile_values: bfloat16 [65536, 128, 128], P(('vp', 'rep')), may hold values from 0 to 0.0014648438
- tile_cols: int32 [65536], P(('vp', 'rep')), may hold values from 0 to 31, as said below
- halo_rows: int32 [256, 4, 4], P(('vp', 'rep')), may hold values from 0 to 15
Outputs:
- scores: bfloat16 [524288, 256], P(('vp', 'rep'))
Inputs may be any that keep to these rules, and one draw needn't show every extreme that they name: `tile_cols`: values below 16 name one of the shard's own row blocks; value 16 + o * 4 + j names the j-th block sent by peer o. Every value occurs on every shard.
All inputs are finite; a program needn't handle non-finite values.
Results may differ from a plain program's by a relative error of at most 0.002.
Values may be sent and summed in bfloat16 or wider, within the bound.
A program may use at most 128 MiB of HBM per device.

v0:
```python
import jax
import jax.numpy as jnp
from jax import lax
from jax.sharding import PartitionSpec as P

ITERS = 3


peer_offsets = (1, -1, 4, -4)


def passed_along(shard, axis, by):
    count = lax.axis_size(axis)
    return lax.ppermute(shard, axis, [(i, (i + by) % count) for i in range(count)])


def total_of_pieces(shard, axis):
    blocks = lax.all_gather(shard, axis)
    return blocks.sum(axis=0)


def copy_for_each(shard, axis):
    count = lax.axis_size(axis)
    return lax.all_to_all(
        jnp.broadcast_to(shard[None], (count, *shard.shape)), axis, 0, 0, tiled=True
    )


def of_everyone(shard, axis):
    everything = copy_for_each(shard, axis)
    return jnp.sum(everything, axis=0)


def local(features, tile_values, tile_cols, halo_rows):
    tile_size = tile_values.shape[1]
    classes = features.shape[1]
    nblocks = features.shape[0] // tile_size
    per_row = tile_values.shape[0] // nblocks
    shards = lax.axis_size("vp") * lax.axis_size("rep")
    vertices = features.shape[0] * shards
    send_lists = halo_rows[0]
    tiles = tile_values.reshape(nblocks, per_row, tile_size, tile_size)
    tile_slots = tile_cols.reshape(nblocks, per_row)
    current = features
    for iteration in range(ITERS):
        own_blocks = current.reshape(nblocks, tile_size, classes)
        halo_blocks = []
        for which in range(4):
            halo_blocks.append(
                passed_along(own_blocks[send_lists[which]], ("vp", "rep"), peer_offsets[which])
            )
        block_table = jnp.concatenate([own_blocks] + halo_blocks, axis=0)
        picked = block_table[tile_slots]
        propagated = jnp.einsum(
            "rtij,rtjc->ric", tiles, picked, preferred_element_type=jnp.float32
        ).reshape(-1, classes)
        blended = 0.9 * propagated + 0.1 * features.astype(jnp.float32)
        local_mass = jnp.sum(blended * blended, axis=0)
        group_mass = total_of_pieces(local_mass, "rep")
        total_mass = of_everyone(group_mass, "vp")
        current = (blended / jnp.sqrt(0.05 + total_mass / vertices)).astype(jnp.bfloat16)
    return current


def solution(mesh):
    return jax.shard_map(
        local,
        mesh=mesh,
        in_specs=(
            P(("vp", "rep"), None),
            P(("vp", "rep"), None, None),
            P(("vp", "rep")),
            P(("vp", "rep"), None, None),
        ),
        out_specs=P(("vp", "rep"), None),
        check_vma=False,
    )
```

profile of v0, /device:TPU:1, one launch (start us, length us, event | category | flops | bytes accessed | tf_op | source)
XLA Modules:
  0.0 222.4 jit_solution(6301716887849608904)
XLA Ops:
  0.9 1.8 gather_fusion.3
  2.6 3.3 %collective-permute-start.3 = (bf16[4,128,256]{2,1,0:T(8,128)(2,1)S(1)}, bf16[4,128,256]{2,1,0:T(8,128)(2,1)}, u32[]{:S(2)}, u32[]{:S(2)}) collective-permute-start(bf16[4,128,256]{2,1,0:T(8,128)(2,1)S(1)} %gather_fusion.3), channel_id=1, source_target_pairs={{0,252},{1,253},{2,254},{3,255},{4,0},{5,1},{6,2},{7,3},{8,4},{9,5... | collective-permute-start | bytes 786440 | tf_op jit(solution)/shard_map/ppermute | solution.py:14
  5.9 2.5 %gather_fusion.1 = bf16[4,128,256]{2,1,0:T(8,128)(2,1)} fusion(bf16[16,128,256]{2,1,0:T(8,128)(2,1)} %bitcast.74, s32[1024]{0:T(1024)S(1)} %pad_clamp_fusion.3), kind=kCustom, calls=%fused_computation.1 | custom fusion | bytes 524304 | tf_op jit(solution)/shard_map/gather | solution.py:50
  8.4 8.4 %collective-permute-start.1 = (bf16[4,128,256]{2,1,0:T(8,128)(2,1)}, bf16[4,128,256]{2,1,0:T(8,128)(2,1)}, u32[]{:S(2)}, u32[]{:S(2)}) collective-permute-start(bf16[4,128,256]{2,1,0:T(8,128)(2,1)} %gather_fusion.1), channel_id=1, source_target_pairs={{0,255},{1,0},{2,1},{3,2},{4,3},{5,4},{6,5},{7,6},{8,7},{9,8},{10,... | collective-permute-start | bytes 786440 | tf_op jit(solution)/shard_map/ppermute | solution.py:14
  16.8 2.5 %gather_fusion = bf16[4,128,256]{2,1,0:T(8,128)(2,1)} fusion(bf16[16,128,256]{2,1,0:T(8,128)(2,1)} %bitcast.75, s32[1024]{0:T(1024)S(1)} %pad_clamp_fusion.4), kind=kCustom, calls=%fused_computation | custom fusion | bytes 524304 | tf_op jit(solution)/shard_map/gather | solution.py:50
  19.3 2.5 %gather_fusion.2 = bf16[4,128,256]{2,1,0:T(8,128)(2,1)} fusion(bf16[16,128,256]{2,1,0:T(8,128)(2,1)} %bitcast.76, s32[1024]{0:T(1024)S(1)} %pad_clamp_fusion.2), kind=kCustom, calls=%fused_computation.2 | custom fusion | bytes 524304 | tf_op jit(solution)/shard_map/gather | solution.py:50
  22.1 7.6 %collective-permute-done = bf16[4,128,256]{2,1,0:T(8,128)(2,1)} collective-permute-done((bf16[4,128,256]{2,1,0:T(8,128)(2,1)}, bf16[4,128,256]{2,1,0:T(8,128)(2,1)}, u32[]{:S(2)}, u32[]{:S(2)}) %collective-permute-start) | collective-permute-done | bytes 262176 | tf_op jit(solution)/shard_map/ppermute | solution.py:14
  33.7 9.7 %gather_fusion.4 = bf16[256,128,256]{2,1,0:T(8,128)(2,1)} fusion(bf16[32,128,256]{2,1,0:T(8,128)(2,1)S(1)} %constant_dynamic-update-slice_fusion, s32[1024]{0:T(1024)S(1)} %pad_clamp_fusion), kind=kCustom, calls=%fused_computation.4 | custom fusion | bytes 33555456 | tf_op jit(solution)/shard_map/gather | solution.py:53
  43.4 10.5 %bitcast_multiply_fusion.2 = f32[16,256,128]{1,2,0:T(8,128)S(1)} fusion(bf16[16,16,128,128]{3,2,1,0:T(8,128)(2,1)} %bitcast.67, bf16[16,16,128,256]{3,2,1,0:T(8,128)(2,1)} %bitcast.71), kind=kOutput, calls=%fused_computation.20 | convolution fusion | flops 2148007936 | bytes 27262976 | tf_op jit(solution)/shard_map/rtij,rtjc->ric/dot_general | solution.py:54
  54.4 5.2 %all-gather.3 = f32[4,1,256]{2,1,0:T(1,128)S(1)} all-gather(f32[1,1,256]{2,1,0:T(1,128)S(1)} %bitcast.88), channel_id=2, replica_groups=mesh['vp'=64,'rep'=4] {'rep'}, dimensions={0}, use_global_device_ids=true | all-gather | bytes 5120 | tf_op jit(solution)/shard_map/all_gather | solution.py:18
  59.7 18.8 %all_to_all.18 = f32[64,1,256]{2,1,0:T(1,128)S(1)} all-to-all(f32[64,1,256]{2,1,0:T(1,128)S(1)} %broadcast_in_dim.6), channel_id=1, replica_groups=mesh['vp'=64,'rep'=4] {'vp'}, dimensions={0} | all-to-all | bytes 131072 | tf_op jit(solution)/shard_map/all_to_all | solution.py:24
  79.9 2.5 %gather_fusion.5 = bf16[4,128,256]{2,1,0:T(8,128)(2,1)} fusion(bf16[16,128,256]{2,1,0:T(8,128)(2,1)} %bitcast.83, s32[1024]{0:T(1024)S(1)} %pad_clamp_fusion.4), kind=kCustom, calls=%fused_computation.5 | custom fusion | bytes 524304 | tf_op jit(solution)/shard_map/gather | solution.py:50
  82.4 1.7 collective-permute-start.4
  84.1 2.5 %gather_fusion.6 = bf16[4,128,256]{2,1,0:T(8,128)(2,1)} fusion(bf16[16,128,256]{2,1,0:T(8,128)(2,1)} %bitcast.84, s32[1024]{0:T(1024)S(1)} %pad_clamp_fusion.3), kind=kCustom, calls=%fused_computation.6 | custom fusion | bytes 524304 | tf_op jit(solution)/shard_map/gather | solution.py:50
  87.8 2.5 %gather_fusion.7 = bf16[4,128,256]{2,1,0:T(8,128)(2,1)} fusion(bf16[16,128,256]{2,1,0:T(8,128)(2,1)} %bitcast.85, s32[1024]{0:T(1024)S(1)} %pad_clamp_fusion.2), kind=kCustom, calls=%fused_computation.7 | custom fusion | bytes 524304 | tf_op jit(solution)/shard_map/gather | solution.py:50
  90.3 1.7 collective-permute-start.6
  93.3 1.8 gather_fusion.8
  95.1 3.0 %collective-permute-start.7 = (bf16[4,128,256]{2,1,0:T(8,128)(2,1)S(1)}, bf16[4,128,256]{2,1,0:T(8,128)(2,1)S(1)}, u32[]{:S(2)}, u32[]{:S(2)}) collective-permute-start(bf16[4,128,256]{2,1,0:T(8,128)(2,1)S(1)} %gather_fusion.8), channel_id=1, source_target_pairs={{0,252},{1,253},{2,254},{3,255},{4,0},{5,1},{6,2},{7,3},{8,4},{9,5... | collective-permute-start | bytes 786440 | tf_op jit(solution)/shard_map/ppermute | solution.py:14
  101.4 9.7 %gather_fusion.9 = bf16[256,128,256]{2,1,0:T(8,128)(2,1)} fusion(bf16[32,128,256]{2,1,0:T(8,128)(2,1)S(1)} %constant_dynamic-update-slice_fusion.5, s32[1024]{0:T(1024)S(1)} %pad_clamp_fusion), kind=kCustom, calls=%fused_computation.9 | custom fusion | bytes 33555456 | tf_op jit(solution)/shard_map/gather | solution.py:53
  111.1 10.5 %bitcast_multiply_fusion.1 = f32[16,256,128]{1,2,0:T(8,128)S(1)} fusion(bf16[16,16,128,128]{3,2,1,0:T(8,128)(2,1)} %bitcast.68, bf16[16,16,128,256]{3,2,1,0:T(8,128)(2,1)} %bitcast.72), kind=kOutput, calls=%fused_computation.19 | convolution fusion | flops 2148007936 | bytes 27262976 | tf_op jit(solution)/shard_map/rtij,rtjc->ric/dot_general | solution.py:54
  122.1 5.2 %all-gather.4 = f32[4,1,256]{2,1,0:T(1,128)S(1)} all-gather(f32[1,1,256]{2,1,0:T(1,128)S(1)} %bitcast.89), channel_id=3, replica_groups=mesh['vp'=64,'rep'=4] {'rep'}, dimensions={0}, use_global_device_ids=true | all-gather | bytes 5120 | tf_op jit(solution)/shard_map/all_gather | solution.py:18
  127.4 22.3 %all_to_all.19 = f32[64,1,256]{2,1,0:T(1,128)S(1)} all-to-all(f32[64,1,256]{2,1,0:T(1,128)S(1)} %broadcast_in_dim.7), channel_id=1, replica_groups=mesh['vp'=64,'rep'=4] {'vp'}, dimensions={0} | all-to-all | bytes 131072 | tf_op jit(solution)/shard_map/all_to_all | solution.py:24
  151.1 2.5 %gather_fusion.10 = bf16[4,128,256]{2,1,0:T(8,128)(2,1)} fusion(bf16[16,128,256]{2,1,0:T(8,128)(2,1)} %bitcast.78, s32[1024]{0:T(1024)S(1)} %pad_clamp_fusion.4), kind=kCustom, calls=%fused_computation.10 | custom fusion | bytes 524304 | tf_op jit(solution)/shard_map/gather | solution.py:50
  155.0 2.5 %gather_fusion.11 = bf16[4,128,256]{2,1,0:T(8,128)(2,1)} fusion(bf16[16,128,256]{2,1,0:T(8,128)(2,1)} %bitcast.79, s32[1024]{0:T(1024)S(1)} %pad_clamp_fusion.3), kind=kCustom, calls=%fused_computation.11 | custom fusion | bytes 524304 | tf_op jit(solution)/shard_map/gather | solution.py:50
  159.0 1.8 gather_fusion.12
  160.8 1.8 collective-permute-start.10
  163.8 2.5 %gather_fusion.13 = bf16[4,128,256]{2,1,0:T(8,128)(2,1)} fusion(bf16[16,128,256]{2,1,0:T(8,128)(2,1)} %bitcast.82, s32[1024]{0:T(1024)S(1)} %pad_clamp_fusion.1), kind=kCustom, calls=%fused_computation.13 | custom fusion | bytes 524304 | tf_op jit(solution)/shard_map/gather | solution.py:50
  166.3 2.9 %collective-permute-start.11 = (bf16[4,128,256]{2,1,0:T(8,128)(2,1)}, bf16[4,128,256]{2,1,0:T(8,128)(2,1)S(1)}, u32[]{:S(2)}, u32[]{:S(2)}) collective-permute-start(bf16[4,128,256]{2,1,0:T(8,128)(2,1)} %gather_fusion.13), channel_id=1, source_target_pairs={{0,252},{1,253},{2,254},{3,255},{4,0},{5,1},{6,2},{7,3},{8,4},{9,5... | collective-permute-start | bytes 786440 | tf_op jit(solution)/shard_map/ppermute | solution.py:14
  172.8 9.7 %gather_fusion.14 = bf16[256,128,256]{2,1,0:T(8,128)(2,1)} fusion(bf16[32,128,256]{2,1,0:T(8,128)(2,1)S(1)} %constant_dynamic-update-slice_fusion.10, s32[1024]{0:T(1024)S(1)} %pad_clamp_fusion), kind=kCustom, calls=%fused_computation.14 | custom fusion | bytes 33555456 | tf_op jit(solution)/shard_map/gather | solution.py:53
  182.5 10.5 %bitcast_multiply_fusion = f32[16,256,128]{1,2,0:T(8,128)S(1)} fusion(bf16[16,16,128,128]{3,2,1,0:T(8,128)(2,1)} %bitcast.69, bf16[16,16,128,256]{3,2,1,0:T(8,128)(2,1)} %bitcast.70), kind=kOutput, calls=%fused_computation.18 | convolution fusion | flops 2148007936 | bytes 27262976 | tf_op jit(solution)/shard_map/rtij,rtjc->ric/dot_general | solution.py:54
  193.5 5.2 %all-gather.5 = f32[4,1,256]{2,1,0:T(1,128)S(1)} all-gather(f32[1,1,256]{2,1,0:T(1,128)S(1)} %bitcast.90), channel_id=4, replica_groups=mesh['vp'=64,'rep'=4] {'rep'}, dimensions={0}, use_global_device_ids=true | all-gather | bytes 5120 | tf_op jit(solution)/shard_map/all_gather | solution.py:18
  198.8 22.3 %all_to_all.20 = f32[64,1,256]{2,1,0:T(1,128)S(1)} all-to-all(f32[64,1,256]{2,1,0:T(1,128)S(1)} %broadcast_in_dim.8), channel_id=1, replica_groups=mesh['vp'=64,'rep'=4] {'vp'}, dimensions={0} | all-to-all | bytes 131072 | tf_op jit(solution)/shard_map/all_to_all | solution.py:24
  (62 shorter events, 24.1 us)
Async XLA Ops:
  0.0 21.9 %copy-start = (bf16[2048,256]{1,0:T(8,128)(2,1)S(1)}, bf16[2048,256]{1,0:T(8,128)(2,1)}, u32[]{:S(2)}) copy-start(bf16[2048,256]{1,0:T(8,128)(2,1)} %param.4) | copy-start | bytes 3145732
  0.0 21.8 %copy-start.1 = (s32[256]{0:T(256)S(1)}, s32[256]{0:T(256)}, u32[]{:S(2)}) copy-start(s32[256]{0:T(256)} %param.6) | copy-start | bytes 3076
  2.6 30.0 %collective-permute-start.3 = (bf16[4,128,256]{2,1,0:T(8,128)(2,1)S(1)}, bf16[4,128,256]{2,1,0:T(8,128)(2,1)}, u32[]{:S(2)}, u32[]{:S(2)}) collective-permute-start(bf16[4,128,256]{2,1,0:T(8,128)(2,1)S(1)} %gather_fusion.3), channel_id=1, source_target_pairs={{0,252},{1,253},{2,254},{3,255},{4,0},{5,1},{6,2},{7,3},{8,4},{9,5... | collective-permute-start | bytes 786440 | tf_op jit(solution)/shard_map/ppermute | solution.py:14
  8.4 22.3 %collective-permute-start.1 = (bf16[4,128,256]{2,1,0:T(8,128)(2,1)}, bf16[4,128,256]{2,1,0:T(8,128)(2,1)}, u32[]{:S(2)}, u32[]{:S(2)}) collective-permute-start(bf16[4,128,256]{2,1,0:T(8,128)(2,1)} %gather_fusion.1), channel_id=1, source_target_pairs={{0,255},{1,0},{2,1},{3,2},{4,3},{5,4},{6,5},{7,6},{8,7},{9,8},{10,... | collective-permute-start | bytes 786440 | tf_op jit(solution)/shard_map/ppermute | solution.py:14
  19.3 10.4 %collective-permute-start = (bf16[4,128,256]{2,1,0:T(8,128)(2,1)}, bf16[4,128,256]{2,1,0:T(8,128)(2,1)}, u32[]{:S(2)}, u32[]{:S(2)}) collective-permute-start(bf16[4,128,256]{2,1,0:T(8,128)(2,1)} %gather_fusion), channel_id=1, source_target_pairs={{0,1},{1,2},{2,3},{3,4},{4,5},{5,6},{6,7},{7,8},{8,9},{9,10},{10,1... | collective-permute-start | bytes 786440 | tf_op jit(solution)/shard_map/ppermute | solution.py:14
  21.8 9.9 %collective-permute-start.2 = (bf16[4,128,256]{2,1,0:T(8,128)(2,1)}, bf16[4,128,256]{2,1,0:T(8,128)(2,1)}, u32[]{:S(2)}, u32[]{:S(2)}) collective-permute-start(bf16[4,128,256]{2,1,0:T(8,128)(2,1)} %gather_fusion.2), channel_id=1, source_target_pairs={{0,4},{1,5},{2,6},{3,7},{4,8},{5,9},{6,10},{7,11},{8,12},{9,13},{1... | collective-permute-start | bytes 786440 | tf_op jit(solution)/shard_map/ppermute | solution.py:14
  82.4 15.7 %collective-permute-start.4 = (bf16[4,128,256]{2,1,0:T(8,128)(2,1)}, bf16[4,128,256]{2,1,0:T(8,128)(2,1)}, u32[]{:S(2)}, u32[]{:S(2)}) collective-permute-start(bf16[4,128,256]{2,1,0:T(8,128)(2,1)} %gather_fusion.5), channel_id=1, source_target_pairs={{0,1},{1,2},{2,3},{3,4},{4,5},{5,6},{6,7},{7,8},{8,9},{9,10},{10,1... | collective-permute-start | bytes 786440 | tf_op jit(solution)/shard_map/ppermute | solution.py:14
  86.6 12.5 %collective-permute-start.5 = (bf16[4,128,256]{2,1,0:T(8,128)(2,1)}, bf16[4,128,256]{2,1,0:T(8,128)(2,1)}, u32[]{:S(2)}, u32[]{:S(2)}) collective-permute-start(bf16[4,128,256]{2,1,0:T(8,128)(2,1)} %gather_fusion.6), channel_id=1, source_target_pairs={{0,255},{1,0},{2,1},{3,2},{4,3},{5,4},{6,5},{7,6},{8,7},{9,8},{10,... | collective-permute-start | bytes 786440 | tf_op jit(solution)/shard_map/ppermute | solution.py:14
  90.3 9.8 %collective-permute-start.6 = (bf16[4,128,256]{2,1,0:T(8,128)(2,1)}, bf16[4,128,256]{2,1,0:T(8,128)(2,1)}, u32[]{:S(2)}, u32[]{:S(2)}) collective-permute-start(bf16[4,128,256]{2,1,0:T(8,128)(2,1)} %gather_fusion.7), channel_id=1, source_target_pairs={{0,4},{1,5},{2,6},{3,7},{4,8},{5,9},{6,10},{7,11},{8,12},{9,13},{1... | collective-permute-start | bytes 786440 | tf_op jit(solution)/shard_map/ppermute | solution.py:14
  95.1 6.3 %collective-permute-start.7 = (bf16[4,128,256]{2,1,0:T(8,128)(2,1)S(1)}, bf16[4,128,256]{2,1,0:T(8,128)(2,1)S(1)}, u32[]{:S(2)}, u32[]{:S(2)}) collective-permute-start(bf16[4,128,256]{2,1,0:T(8,128)(2,1)S(1)} %gather_fusion.8), channel_id=1, source_target_pairs={{0,252},{1,253},{2,254},{3,255},{4,0},{5,1},{6,2},{7,3},{8,4},{9,5... | collective-permute-start | bytes 786440 | tf_op jit(solution)/shard_map/ppermute | solution.py:14
  153.5 15.8 %collective-permute-start.8 = (bf16[4,128,256]{2,1,0:T(8,128)(2,1)}, bf16[4,128,256]{2,1,0:T(8,128)(2,1)}, u32[]{:S(2)}, u32[]{:S(2)}) collective-permute-start(bf16[4,128,256]{2,1,0:T(8,128)(2,1)} %gather_fusion.10), channel_id=1, source_target_pairs={{0,1},{1,2},{2,3},{3,4},{4,5},{5,6},{6,7},{7,8},{8,9},{9,10},{10,1... | collective-permute-start | bytes 786440 | tf_op jit(solution)/shard_map/ppermute | solution.py:14
  157.5 12.8 %collective-permute-start.9 = (bf16[4,128,256]{2,1,0:T(8,128)(2,1)}, bf16[4,128,256]{2,1,0:T(8,128)(2,1)}, u32[]{:S(2)}, u32[]{:S(2)}) collective-permute-start(bf16[4,128,256]{2,1,0:T(8,128)(2,1)} %gather_fusion.11), channel_id=1, source_target_pairs={{0,255},{1,0},{2,1},{3,2},{4,3},{5,4},{6,5},{7,6},{8,7},{9,8},{10,... | collective-permute-start | bytes 786440 | tf_op jit(solution)/shard_map/ppermute | solution.py:14
  160.8 10.5 %collective-permute-start.10 = (bf16[4,128,256]{2,1,0:T(8,128)(2,1)S(1)}, bf16[4,128,256]{2,1,0:T(8,128)(2,1)}, u32[]{:S(2)}, u32[]{:S(2)}) collective-permute-start(bf16[4,128,256]{2,1,0:T(8,128)(2,1)S(1)} %gather_fusion.12), channel_id=1, source_target_pairs={{0,4},{1,5},{2,6},{3,7},{4,8},{5,9},{6,10},{7,11},{8,12},{9,13},{1... | collective-permute-start | bytes 786440 | tf_op jit(solution)/shard_map/ppermute | solution.py:14
  166.3 6.4 %collective-permute-start.11 = (bf16[4,128,256]{2,1,0:T(8,128)(2,1)}, bf16[4,128,256]{2,1,0:T(8,128)(2,1)S(1)}, u32[]{:S(2)}, u32[]{:S(2)}) collective-permute-start(bf16[4,128,256]{2,1,0:T(8,128)(2,1)} %gather_fusion.13), channel_id=1, source_target_pairs={{0,252},{1,253},{2,254},{3,255},{4,0},{5,1},{6,2},{7,3},{8,4},{9,5... | collective-permute-start | bytes 786440 | tf_op jit(solution)/shard_map/ppermute | solution.py:14
where the time goes:
time: 224 us; the launch traced here: 222 us
  blocking collectives  79.1 us (35%)
  local copies, waits for them, and re-layouts  69.7 us (31%)
  matrix products  31.5 us (14%)
  starting transfers between devices  27 us (12%)
  waiting for transfers between devices  8.5 us (4%)
  other arithmetic  6.41 us (3%)
    all_to_all x3, blocking collectives, copy_for_each(): lax.all_to_all(jnp.broadcast_to(shard[None], (count, *shard.shape)), axis...  63.4 us
    dot_general x3, matrix products, local(): jnp.einsum('rtij,rtjc->ric', tiles, picked, preferred_element_type=jnp.fl...  31.5 us
    gather x3, local copies, waits for them, and re-layouts, local(): picked = block_table[tile_slots]  29.2 us
    gather x12, local copies, waits for them, and re-layouts, local(): own_blocks[send_lists[which]]  27.8 us
    ppermute x12, starting transfers between devices, passed_along(): lax.ppermute(shard, axis, [(i, (i + by) % count) for i in range(count)])  27 us
    all_gather x3, blocking collectives, total_of_pieces(): blocks = lax.all_gather(shard, axis)  15.7 us
    unnamed x16, local copies, waits for them, and re-layouts  11.4 us
    ppermute x12, waiting for transfers between devices, passed_along(): lax.ppermute(shard, axis, [(i, (i + by) % count) for i in range(count)])  8.5 us
  transfers between devices with their start and end apart: 12, of which 3 were waited for; matrix products, arithmetic and copies ran while one was open for 15% of the time, Pallas kernels for 0%

commit v1 on v0

v1 whole, which is shorter than its diff:
```python
import jax
import jax.numpy as jnp
from jax import lax
from jax.experimental import pallas as pl
from jax.experimental.pallas import tpu as pltpu
from jax.sharding import PartitionSpec as P

ITERS = 3
TILE = 128
NB = 16
SLOTS = 4
PEERS = 4
KEEP, TELEPORT = 0.9, 0.1
MESH = pl.DeviceIdType.MESH
HALF = 128


def kernel(
    feat_hbm, tiles_hbm, cols, halo, out,
    fbuf, tiles, tab0, tab1, tab2, snd0, snd1, snd2, u1, u2, u3,
    gram, early1, early2, late1, late2,
    load_sem, halo_send, halo_recv, ar_send, ar_recv,
):
    vp, rep = lax.axis_index("vp"), lax.axis_index("rep")
    nvp, nrep = lax.axis_size("vp"), lax.axis_size("rep")
    shards = nvp * nrep
    me = vp * nrep + rep
    vertices = shards * NB * TILE
    plane = vp // 16 * nrep + rep
    column = vp % 16

    def plane_member(i):
        return (i // nrep * 16 + vp % 16, i % nrep)

    def column_member(i):
        return (vp // 16 * 16 + i, rep)

    def peer(o):
        shift = (1, -1, 4, -4)[o]
        d = lax.rem(me + shift + shards, shards)
        return (d // nrep, d % nrep)

    loads = [
        pltpu.make_async_copy(feat_hbm, fbuf, load_sem.at[0]),
        pltpu.make_async_copy(feat_hbm, tab0.at[pl.ds(0, NB)], load_sem.at[1]),
        pltpu.make_async_copy(tiles_hbm, tiles, load_sem.at[2]),
    ]
    for copy in loads:
        copy.start()

    barrier = pltpu.get_barrier_semaphore()
    for o in range(PEERS):
        pl.semaphore_signal(barrier, inc=1, device_id=peer(o), device_id_type=MESH)
    for k in range(1, 16):
        pl.semaphore_signal(
            barrier, inc=1, device_id=plane_member((plane + k) % 16), device_id_type=MESH)
        pl.semaphore_signal(
            barrier, inc=1, device_id=column_member((column + k) % 16), device_id_type=MESH)
    gram[...] = jnp.zeros_like(gram)

    snd, tab = (snd0, snd1, snd2), (tab0, tab1, tab2)

    def halo_copy(step, o, j):
        i = o * SLOTS + j
        return pltpu.make_async_remote_copy(
            src_ref=snd[step].at[i],
            dst_ref=tab[step].at[NB + i],
            send_sem=halo_send.at[step, i],
            recv_sem=halo_recv.at[step, i],
            device_id=peer(o),
            device_id_type=MESH,
        )

    def row_block(table, r):
        total = None
        for p in range(NB // 2):
            t = r * NB + 2 * p
            lhs = jnp.concatenate([tiles[t], tiles[t + 1]], axis=1)
            rhs = jnp.concatenate([table[cols[t]], table[cols[t + 1]]], axis=0)
            term = jnp.dot(lhs, rhs, preferred_element_type=jnp.float32)
            total = term if total is None else total + term
        return total

    def fold(x):
        return jnp.sum(x.reshape(NB, 8, x.shape[-1]), axis=0)

    loads[0].wait()
    for j in range(SLOTS):
        for o in range(PEERS):
            snd0[o * SLOTS + j] = fbuf[halo[0, o, j]]
    pl.semaphore_wait(barrier, PEERS + 30)
    for j in range(SLOTS):
        for o in range(PEERS):
            halo_copy(0, o, j).start()
    loads[1].wait()
    loads[2].wait()

    def wait_halo(step):
        for o in range(PEERS):
            for j in range(SLOTS):
                halo_copy(step, o, j).wait_recv()

    def send_pass(step):
        def body(j, _):
            for o in range(PEERS):
                snd[step][o * SLOTS + j] = row_block(tab[step - 1], halo[0, o, j]).astype(jnp.bfloat16)
                halo_copy(step, o, j).start()
            return 0

        lax.fori_loop(0, SLOTS, body, 0)

    def own_pass(step, keep, others, first):
        def body(q, _):
            for part in range(4):
                r = q * 4 + part
                u = row_block(tab[step - 1], r)
                keep[r] = u
                if step < ITERS:
                    tab[step][r] = u.astype(jnp.bfloat16)
                for i, other in enumerate(others):
                    gram[first + i] += fold(other[r].astype(jnp.float32) * u)
                gram[first + len(others)] += fold(u * u)
            return 0

        lax.fori_loop(0, 4, body, 0)

    def pack(buf, mine, first, count):
        for i in range(count):
            row = jnp.sum(gram[first + i], axis=0, keepdims=True)
            for h in range(2):
                buf[mine, pl.ds(2 * i + h, 1), :] = row[:, h * HALF:(h + 1) * HALF]

    def stage(number, buf, mine, member):
        copies = []
        for k in range(1, 16):
            copies.append(pltpu.make_async_remote_copy(
                src_ref=buf.at[mine],
                dst_ref=buf.at[mine],
                send_sem=ar_send.at[number, k - 1],
                recv_sem=ar_recv.at[number, k - 1],
                device_id=member((mine + k) % 16),
                device_id_type=MESH,
            ))
        return copies

    def total_of(buf):
        total = buf[0]
        for i in range(1, 16):
            total = total + buf[i]
        return total

    wait_halo(0)
    send_pass(1)
    def ff_body(r, _):
        f = fbuf[r].astype(jnp.float32)
        gram[0] += fold(f * f)
        return 0
    lax.fori_loop(0, NB, ff_body, 0)
    own_pass(1, u1, (fbuf,), 1)
    wait_halo(1)
    send_pass(2)
    own_pass(2, u2, (fbuf, u1), 3)
    early1[plane, pl.ds(12, 4), :] = jnp.zeros((4, HALF), jnp.float32)
    pack(early1, plane, 0, 6)
    early_a = stage(0, early1, plane, plane_member)
    for copy in early_a:
        copy.start()
    wait_halo(2)
    for copy in early_a:
        copy.wait_recv()
    early2[column] = total_of(early1)
    early_b = stage(1, early2, column, column_member)
    for copy in early_b:
        copy.start()
    own_pass(3, u3, (fbuf, u1, u2), 6)
    pack(late1, plane, 6, 4)
    late_a = stage(2, late1, plane, plane_member)
    for copy in late_a:
        copy.start()
    for copy in early_b:
        copy.wait_recv()
    early = total_of(early2)
    for copy in late_a:
        copy.wait_recv()
    late2[column] = total_of(late1)
    late_b = stage(3, late2, column, column_member)
    for copy in late_b:
        copy.start()

    def row(block, i):
        return jnp.concatenate([block[2 * i:2 * i + 1], block[2 * i + 1:2 * i + 2]], axis=1)

    a, b = KEEP, TELEPORT
    ff, f1, g11, f2, g12, g22 = (row(early, i) for i in range(6))
    mass1 = a * a * g11 + 2 * a * b * f1 + b * b * ff
    s1 = 1.0 / jnp.sqrt(0.05 + mass1 / vertices)
    w22 = a * a * g22 + 2 * a * b * g12 + b * b * g11
    w2f = a * f2 + b * f1
    mass2 = (a * s1) * (a * s1) * w22 + 2 * a * b * s1 * w2f + b * b * ff
    s2 = 1.0 / jnp.sqrt(0.05 + mass2 / vertices)
    c3 = a * a * a * s1 * s2
    c2 = a * a * b * s1 * s2
    c1 = a * b * s2

    def blend(r, _):
        u3[r] = c3 * u3[r] + c2 * u2[r] + c1 * u1[r] + b * fbuf[r].astype(jnp.float32)
        return 0

    lax.fori_loop(0, NB, blend, 0)
    for copy in late_b:
        copy.wait_recv()
    late = total_of(late2)
    f3, g13, g23, g33 = (row(late, i) for i in range(4))
    mass3 = (
        c3 * c3 * g33 + c2 * c2 * g22 + c1 * c1 * g11 + b * b * ff
        + 2 * (c3 * c2 * g23 + c3 * c1 * g13 + c2 * c1 * g12)
        + 2 * b * (c3 * f3 + c2 * f2 + c1 * f1)
    )
    s3 = 1.0 / jnp.sqrt(0.05 + mass3 / vertices)

    def finish(r, _):
        out[r] = (u3[r] * s3).astype(jnp.bfloat16)
        return 0

    lax.fori_loop(0, NB, finish, 0)

    for step in range(ITERS):
        for o in range(PEERS):
            for j in range(SLOTS):
                halo_copy(step, o, j).wait_send()
    for copy in early_a + early_b + late_a + late_b:
        copy.wait_send()


def local(features, tile_values, tile_cols, halo_rows):
    classes = features.shape[1]
    rows = (NB, TILE, classes)
    anywhere = pl.BlockSpec(memory_space=pl.ANY)
    scalars = pl.BlockSpec(memory_space=pltpu.SMEM)
    table = pltpu.VMEM((2 * NB, TILE, classes), jnp.bfloat16)
    blocks = pltpu.VMEM(rows, jnp.bfloat16)
    wide = pltpu.VMEM(rows, jnp.float32)
    scores = pl.pallas_call(
        kernel,
        out_shape=jax.ShapeDtypeStruct(rows, jnp.bfloat16),
        in_specs=[anywhere, anywhere, scalars, scalars],
        out_specs=pl.BlockSpec(memory_space=pltpu.VMEM),
        scratch_shapes=[
            blocks,
            pltpu.VMEM(tile_values.shape, jnp.bfloat16),
            table, table, table,
            blocks, blocks, blocks,
            wide, wide, wide,
            pltpu.VMEM((10, 8, classes), jnp.float32),
            pltpu.VMEM((16, 16, HALF), jnp.float32),
            pltpu.VMEM((16, 16, HALF), jnp.float32),
            pltpu.VMEM((16, 8, HALF), jnp.float32),
            pltpu.VMEM((16, 8, HALF), jnp.float32),
            pltpu.SemaphoreType.DMA((3,)),
            pltpu.SemaphoreType.DMA((ITERS, NB)),
            pltpu.SemaphoreType.DMA((ITERS, NB)),
            pltpu.SemaphoreType.DMA((4, 15)),
            pltpu.SemaphoreType.DMA((4, 15)),
        ],
        compiler_params=pltpu.CompilerParams(
            collective_id=0, has_side_effects=True, vmem_limit_bytes=40 * 1024 * 1024
        ),
        name="propagate",
    )(features.reshape(rows), tile_values, tile_cols, halo_rows)
    return scores.reshape(features.shape)


def solution(mesh):
    return jax.shard_map(
        local,
        mesh=mesh,
        in_specs=(
            P(("vp", "rep"), None),
            P(("vp", "rep"), None, None),
            P(("vp", "rep")),
            P(("vp", "rep"), None, None),
        ),
        out_specs=P(("vp", "rep"), None),
        check_vma=False,
    )
```

time: 224 us -> 68.5 us (0.31)
  blocking collectives: 79.1 us -> 0 us
  local copies, waits for them, and re-layouts: 69.7 us -> 6.94 us
  Pallas kernels: 0 us -> 61.4 us
  matrix products: 31.5 us -> 0 us
  starting transfers between devices: 27 us -> 0 us
  waiting for transfers between devices: 8.5 us -> 0 us
  other arithmetic: 6.41 us -> 0 us
    all_to_all x3 -> x0, blocking collectives: 63.4 us -> none  [copy_for_each(): lax.all_to_all(jnp.broadcast_to(shard[None], (count, *shard.shape)), axis...]
    pallas_call x0 -> x1, Pallas kernels: none -> 61.4 us  [local(): pl.pallas_call(kernel, out_shape=jax.ShapeDtypeStruct(rows, jnp.bfloat16)...]
    gather x15 -> x0, local copies, waits for them, and re-layouts: 57 us -> none  [the longest x3 29.2 us: local(): picked = block_table[tile_slots]]
    dot_general x3 -> x0, matrix products: 31.5 us -> none  [local(): jnp.einsum('rtij,rtjc->ric', tiles, picked, preferred_element_type=jnp.fl...]
    ppermute x12 -> x0, starting transfers between devices: 27 us -> none  [passed_along(): lax.ppermute(shard, axis, [(i, (i + by) % count) for i in range(count)])]
    all_gather x3 -> x0, blocking collectives: 15.7 us -> none  [total_of_pieces(): blocks = lax.all_gather(shard, axis)]
    ppermute x12 -> x0, waiting for transfers between devices: 8.5 us -> none  [passed_along(): lax.ppermute(shard, axis, [(i, (i + by) % count) for i in range(count)])]
    unnamed x16 -> x9, local copies, waits for them, and re-layouts: 11.4 us -> 6.94 us
  transfers between devices with their start and end apart: 12 -> 0, of which waited for: 3 -> 0; matrix products, arithmetic and copies ran while one was open for 15% -> 0% of each run, Pallas kernels for 0% -> 0%
where the time goes in v1:
time: 68.5 us; the launch traced here: 68.3 us
  Pallas kernels  61.4 us (90%)
  local copies, waits for them, and re-layouts  6.94 us (10%)
    pallas_call x1, Pallas kernels, local(): pl.pallas_call(kernel, out_shape=jax.ShapeDtypeStruct(rows, jnp.bfloat16)...  61.4 us
    unnamed x9, local copies, waits for them, and re-layouts  6.94 us

profile of v1, /device:TPU:1, one launch (start us, length us, event | category | flops | bytes accessed | tf_op | source)
XLA Modules:
  0.0 68.3 jit_solution(6538206019651973125)
XLA Ops:
  0.0 0.0 copy-start
  0.0 3.4 %copy-done = bf16[256,128,128]{2,1,0:T(8,128)(2,1)S(1)} copy-done((bf16[256,128,128]{2,1,0:T(8,128)(2,1)S(1)}, bf16[256,128,128]{2,1,0:T(8,128)(2,1)}, u32[]{:S(2)}) %copy-start) | copy-done | bytes 8388632
  3.4 0.0 copy-start.1
  3.4 1.2 %copy-done.1 = bf16[2048,256]{1,0:T(8,128)(2,1)S(1)} copy-done((bf16[2048,256]{1,0:T(8,128)(2,1)S(1)}, bf16[2048,256]{1,0:T(8,128)(2,1)}, u32[]{:S(2)}) %copy-start.1) | copy-done | bytes 1048600
  4.6 0.0 copy-start.2
  4.6 0.7 copy-done.2
  5.3 0.0 copy-start.3
  5.3 0.7 copy-done.3
  6.0 61.4 %propagate.1 = bf16[16,128,256]{2,1,0:T(8,128)(2,1)S(1)} custom-call(bf16[16,128,256]{2,1,0:T(8,128)(2,1)S(1)} %bitcast.3, bf16[256,128,128]{2,1,0:T(8,128)(2,1)S(1)} %copy-done, s32[256]{0:T(256)S(1)} %copy-done.3, s32[1,4,4]{2,1,0:T(4,128)S(1)} %copy-done.2), custom_call_target="tpu_custom_call" | custom-call | tf_op jit(solution)/shard_map/propagate/pallas_call | solution.py:243
  67.3 1.0 %copy.6 = bf16[2048,256]{1,0:T(8,128)(2,1)} copy(bf16[2048,256]{1,0:T(8,128)(2,1)S(1)} %bitcast.2) | data formatting | bytes 2097152
Async XLA Ops:
  0.0 3.4 %copy-start = (bf16[256,128,128]{2,1,0:T(8,128)(2,1)S(1)}, bf16[256,128,128]{2,1,0:T(8,128)(2,1)}, u32[]{:S(2)}) copy-start(bf16[256,128,128]{2,1,0:T(8,128)(2,1)} %tiles_hbm.1) | copy-start | bytes 25165828
  3.4 1.2 %copy-start.1 = (bf16[2048,256]{1,0:T(8,128)(2,1)S(1)}, bf16[2048,256]{1,0:T(8,128)(2,1)}, u32[]{:S(2)}) copy-start(bf16[2048,256]{1,0:T(8,128)(2,1)} %param.4) | copy-start | bytes 3145732
  4.6 0.7 copy-start.2
  5.3 0.7 copy-start.3

commit v2 on v1

--- a/solution.py
+++ b/solution.py
@@ -16,8 +16,8 @@
 
 
 def kernel(
-    feat_hbm, tiles_hbm, cols, halo, out,
-    fbuf, tiles, tab0, tab1, tab2, snd0, snd1, snd2, u1, u2, u3,
+    feat_hbm, tiles_hbm, cols_hbm, halo_hbm, out,
+    cols, halo, fbuf, tiles, tab0, tab1, tab2, snd0, snd1, snd2, u1, u2, u3,
     gram, early1, early2, late1, late2,
     load_sem, halo_send, halo_recv, ar_send, ar_recv,
 ):
@@ -35,18 +35,24 @@
     def column_member(i):
         return (vp // 16 * 16 + i, rep)
 
+    core = vp % 2
+
     def peer(o):
-        shift = (1, -1, 4, -4)[o]
+        shift = (1 - o % 2 * 2) * (1 + o // 2 * 3)
         d = lax.rem(me + shift + shards, shards)
         return (d // nrep, d % nrep)
+
+    leading, staying, trailing, across = 1 - core, 2 + core, core, 3 - core
 
     loads = [
         pltpu.make_async_copy(feat_hbm, fbuf, load_sem.at[0]),
         pltpu.make_async_copy(feat_hbm, tab0.at[pl.ds(0, NB)], load_sem.at[1]),
         pltpu.make_async_copy(tiles_hbm, tiles, load_sem.at[2]),
+        pltpu.make_async_copy(cols_hbm, cols, load_sem.at[3]),
+        pltpu.make_async_copy(halo_hbm, halo, load_sem.at[4]),
     ]
-    for copy in loads:
-        copy.start()
+    for i in (4, 0, 3, 1, 2):
+        loads[i].start()
 
     barrier = pltpu.get_barrier_semaphore()
     for o in range(PEERS):
@@ -84,16 +90,20 @@
     def fold(x):
         return jnp.sum(x.reshape(NB, 8, x.shape[-1]), axis=0)
 
+    loads[4].wait()
     loads[0].wait()
     for j in range(SLOTS):
         for o in range(PEERS):
             snd0[o * SLOTS + j] = fbuf[halo[0, o, j]]
     pl.semaphore_wait(barrier, PEERS + 30)
+    for o in (leading, staying):
+        for j in range(SLOTS):
+            halo_copy(0, o, j).start()
     for j in range(SLOTS):
-        for o in range(PEERS):
+        for o in (trailing, across):
             halo_copy(0, o, j).start()
-    loads[1].wait()
-    loads[2].wait()
+    for i in (1, 2, 3):
+        loads[i].wait()
 
     def wait_halo(step):
         for o in range(PEERS):
@@ -101,13 +111,25 @@
                 halo_copy(step, o, j).wait_recv()
 
     def send_pass(step):
-        def body(j, _):
-            for o in range(PEERS):
-                snd[step][o * SLOTS + j] = row_block(tab[step - 1], halo[0, o, j]).astype(jnp.bfloat16)
-                halo_copy(step, o, j).start()
+        def send(o, j):
+            i = o * SLOTS + j
+            snd[step][i] = row_block(tab[step - 1], halo[0, o, j]).astype(jnp.bfloat16)
+            halo_copy(step, o, j).start()
+
+        def one(o):
+            def body(j, _):
+                send(o, j)
+                return 0
+            lax.fori_loop(0, SLOTS, body, 0)
+
+        def two(j, _):
+            send(trailing, j)
+            send(across, j)
             return 0
 
-        lax.fori_loop(0, SLOTS, body, 0)
+        one(leading)
+        one(staying)
+        lax.fori_loop(0, SLOTS, two, 0)
 
     def own_pass(step, keep, others, first):
         def body(q, _):
@@ -225,8 +247,8 @@
     lax.fori_loop(0, NB, finish, 0)
 
     for step in range(ITERS):
-        for o in range(PEERS):
-            for j in range(SLOTS):
+        for j in range(SLOTS):
+            for o in range(PEERS):
                 halo_copy(step, o, j).wait_send()
     for copy in early_a + early_b + late_a + late_b:
         copy.wait_send()
@@ -235,17 +257,22 @@
 def local(features, tile_values, tile_cols, halo_rows):
     classes = features.shape[1]
     rows = (NB, TILE, classes)
-    anywhere = pl.BlockSpec(memory_space=pl.ANY)
-    scalars = pl.BlockSpec(memory_space=pltpu.SMEM)
+    anywhere = pl.BlockSpec(memory_space=pltpu.HBM)
     table = pltpu.VMEM((2 * NB, TILE, classes), jnp.bfloat16)
     blocks = pltpu.VMEM(rows, jnp.bfloat16)
     wide = pltpu.VMEM(rows, jnp.float32)
+    inputs = [
+        pltpu.with_memory_space_constraint(v, pltpu.HBM)
+        for v in (features.reshape(rows), tile_values, tile_cols, halo_rows)
+    ]
     scores = pl.pallas_call(
         kernel,
         out_shape=jax.ShapeDtypeStruct(rows, jnp.bfloat16),
-        in_specs=[anywhere, anywhere, scalars, scalars],
+        in_specs=[anywhere] * 4,
         out_specs=pl.BlockSpec(memory_space=pltpu.VMEM),
         scratch_shapes=[
+            pltpu.SMEM(tile_cols.shape, jnp.int32),
+            pltpu.SMEM(halo_rows.shape, jnp.int32),
             blocks,
             pltpu.VMEM(tile_values.shape, jnp.bfloat16),
             table, table, table,
@@ -256,7 +283,7 @@
             pltpu.VMEM((16, 16, HALF), jnp.float32),
             pltpu.VMEM((16, 8, HALF), jnp.float32),
             pltpu.VMEM((16, 8, HALF), jnp.float32),
-            pltpu.SemaphoreType.DMA((3,)),
+            pltpu.SemaphoreType.DMA((5,)),
             pltpu.SemaphoreType.DMA((ITERS, NB)),
             pltpu.SemaphoreType.DMA((ITERS, NB)),
             pltpu.SemaphoreType.DMA((4, 15)),
@@ -266,7 +293,7 @@
             collective_id=0, has_side_effects=True, vmem_limit_bytes=40 * 1024 * 1024
         ),
         name="propagate",
-    )(features.reshape(rows), tile_values, tile_cols, halo_rows)
+    )(*inputs)
     return scores.reshape(features.shape)
 
 

time: 68.5 us -> 59.3 us (0.87)
  local copies, waits for them, and re-layouts: 6.94 us -> 0.97 us
  Pallas kernels: 61.4 us -> 58.2 us
    unnamed x9 -> x1, local copies, waits for them, and re-layouts: 6.94 us -> 0.97 us
    pallas_call x1, Pallas kernels: 61.4 us -> 58.2 us  [local(): pl.pallas_call(kernel, out_shape=jax.ShapeDtypeStruct(rows, jnp.bfloat16)...]
where the time goes in v2:
time: 59.3 us; the launch traced here: 59.2 us
  Pallas kernels  58.2 us (98%)
  local copies, waits for them, and re-layouts  0.97 us (2%)
    pallas_call x1, Pallas kernels, local(): pl.pallas_call(kernel, out_shape=jax.ShapeDtypeStruct(rows, jnp.bfloat16)...  58.2 us

profile of v2, /device:TPU:1, one launch (start us, length us, event | category | flops | bytes accessed | tf_op | source)
XLA Modules:
  0.0 59.2 jit_solution(12049850349045599184)
XLA Ops:
  0.0 58.2 %propagate.1 = bf16[16,128,256]{2,1,0:T(8,128)(2,1)S(1)} custom-call(bf16[16,128,256]{2,1,0:T(8,128)(2,1)} %bitcast.3, bf16[256,128,128]{2,1,0:T(8,128)(2,1)} %tiles_hbm.1, s32[256]{0:T(256)} %cols_hbm.1, s32[1,4,4]{2,1,0:T(4,128)} %halo_hbm.1), custom_call_target="tpu_custom_call" | custom-call | tf_op jit(solution)/shard_map/propagate/pallas_call | solution.py:268
  58.3 1.0 %copy.6 = bf16[2048,256]{1,0:T(8,128)(2,1)} copy(bf16[2048,256]{1,0:T(8,128)(2,1)S(1)} %bitcast.2) | data formatting | bytes 2097152

commit v3 on v2

--- a/solution.py
+++ b/solution.py
@@ -42,7 +42,7 @@
         d = lax.rem(me + shift + shards, shards)
         return (d // nrep, d % nrep)
 
-    leading, staying, trailing, across = 1 - core, 2 + core, core, 3 - core
+    leading, across, trailing, staying = 1 - core, 3 - core, core, 2 + core
 
     loads = [
         pltpu.make_async_copy(feat_hbm, fbuf, load_sem.at[0]),
@@ -96,11 +96,8 @@
         for o in range(PEERS):
             snd0[o * SLOTS + j] = fbuf[halo[0, o, j]]
     pl.semaphore_wait(barrier, PEERS + 30)
-    for o in (leading, staying):
+    for o in (leading, across, trailing, staying):
         for j in range(SLOTS):
-            halo_copy(0, o, j).start()
-    for j in range(SLOTS):
-        for o in (trailing, across):
             halo_copy(0, o, j).start()
     for i in (1, 2, 3):
         loads[i].wait()
@@ -122,14 +119,8 @@
                 return 0
             lax.fori_loop(0, SLOTS, body, 0)
 
-        def two(j, _):
-            send(trailing, j)
-            send(across, j)
-            return 0
-
-        one(leading)
-        one(staying)
-        lax.fori_loop(0, SLOTS, two, 0)
+        for o in (leading, across, trailing, staying):
+            one(o)
 
     def own_pass(step, keep, others, first):
         def body(q, _):
@@ -188,41 +179,51 @@
     for copy in early_a:
         copy.start()
     wait_halo(2)
+    own_pass(3, u3, (fbuf, u1, u2), 6)
+    pack(late1, plane, 6, 4)
+    late_a = stage(2, late1, plane, plane_member)
+    for copy in late_a:
+        copy.start()
     for copy in early_a:
         copy.wait_recv()
     early2[column] = total_of(early1)
     early_b = stage(1, early2, column, column_member)
     for copy in early_b:
         copy.start()
-    own_pass(3, u3, (fbuf, u1, u2), 6)
-    pack(late1, plane, 6, 4)
-    late_a = stage(2, late1, plane, plane_member)
-    for copy in late_a:
-        copy.start()
     for copy in early_b:
         copy.wait_recv()
     early = total_of(early2)
+
+    def row(block, i):
+        return jnp.concatenate([block[2 * i:2 * i + 1], block[2 * i + 1:2 * i + 2]], axis=1)
+
+    def scale_of(mass):
+        return 1.0 / jnp.sqrt(0.05 + mass / vertices)
+
+    a, b = KEEP, TELEPORT
+    ff, f1, g11, f2, g12, g22 = (row(early, i) for i in range(6))
+    s1 = scale_of(a * a * g11 + 2 * a * b * f1 + b * b * ff)
+    w22 = a * a * g22 + 2 * a * b * g12 + b * b * g11
+    w2f = a * f2 + b * f1
+    s2 = scale_of((a * s1) * (a * s1) * w22 + 2 * a * b * s1 * w2f + b * b * ff)
+    c3 = a * a * a * s1 * s2
+    c2 = a * a * b * s1 * s2
+    c1 = a * b * s2
+
     for copy in late_a:
         copy.wait_recv()
-    late2[column] = total_of(late1)
+    part = total_of(late1)
+    f3, g13, g23, g33 = (row(part, i) for i in range(4))
+    part = c3 * c3 * g33 + 2 * c3 * (c2 * g23 + c1 * g13 + b * f3)
+    for h in range(2):
+        late2[column, pl.ds(h, 1), :] = part[:, h * HALF:(h + 1) * HALF]
     late_b = stage(3, late2, column, column_member)
     for copy in late_b:
         copy.start()
-
-    def row(block, i):
-        return jnp.concatenate([block[2 * i:2 * i + 1], block[2 * i + 1:2 * i + 2]], axis=1)
-
-    a, b = KEEP, TELEPORT
-    ff, f1, g11, f2, g12, g22 = (row(early, i) for i in range(6))
-    mass1 = a * a * g11 + 2 * a * b * f1 + b * b * ff
-    s1 = 1.0 / jnp.sqrt(0.05 + mass1 / vertices)
-    w22 = a * a * g22 + 2 * a * b * g12 + b * b * g11
-    w2f = a * f2 + b * f1
-    mass2 = (a * s1) * (a * s1) * w22 + 2 * a * b * s1 * w2f + b * b * ff
-    s2 = 1.0 / jnp.sqrt(0.05 + mass2 / vertices)
-    c3 = a * a * a * s1 * s2
-    c2 = a * a * b * s1 * s2
-    c1 = a * b * s2
+    known = (
+        c2 * c2 * g22 + c1 * c1 * g11 + b * b * ff
+        + 2 * c2 * (c1 * g12 + b * f2) + 2 * b * c1 * f1
+    )
 
     def blend(r, _):
         u3[r] = c3 * u3[r] + c2 * u2[r] + c1 * u1[r] + b * fbuf[r].astype(jnp.float32)
@@ -231,14 +232,7 @@
     lax.fori_loop(0, NB, blend, 0)
     for copy in late_b:
         copy.wait_recv()
-    late = total_of(late2)
-    f3, g13, g23, g33 = (row(late, i) for i in range(4))
-    mass3 = (
-        c3 * c3 * g33 + c2 * c2 * g22 + c1 * c1 * g11 + b * b * ff
-        + 2 * (c3 * c2 * g23 + c3 * c1 * g13 + c2 * c1 * g12)
-        + 2 * b * (c3 * f3 + c2 * f2 + c1 * f1)
-    )
-    s3 = 1.0 / jnp.sqrt(0.05 + mass3 / vertices)
+    s3 = scale_of(known + row(total_of(late2), 0))
 
     def finish(r, _):
         out[r] = (u3[r] * s3).astype(jnp.bfloat16)
@@ -282,7 +276,7 @@
             pltpu.VMEM((16, 16, HALF), jnp.float32),
             pltpu.VMEM((16, 16, HALF), jnp.float32),
             pltpu.VMEM((16, 8, HALF), jnp.float32),
-            pltpu.VMEM((16, 8, HALF), jnp.float32),
+            pltpu.VMEM((16, 2, HALF), jnp.float32),
             pltpu.SemaphoreType.DMA((5,)),
             pltpu.SemaphoreType.DMA((ITERS, NB)),
             pltpu.SemaphoreType.DMA((ITERS, NB)),

time: 59.3 us -> 57.9 us (0.976)
  Pallas kernels: 58.2 us -> 56.8 us
    pallas_call x1, Pallas kernels: 58.2 us -> 56.8 us  [local(): pl.pallas_call(kernel, out_shape=jax.ShapeDtypeStruct(rows, jnp.bfloat16)...]
where the time goes in v3:
time: 57.9 us; the launch traced here: 57.8 us
  Pallas kernels  56.8 us (98%)
  local copies, waits for them, and re-layouts  0.97 us (2%)
    pallas_call x1, Pallas kernels, local(): pl.pallas_call(kernel, out_shape=jax.ShapeDtypeStruct(rows, jnp.bfloat16)...  56.8 us

profile of v3, /device:TPU:1, one launch (start us, length us, event | category | flops | bytes accessed | tf_op | source)
XLA Modules:
  0.0 57.8 jit_solution(11814021880075398045)
XLA Ops:
  0.0 56.8 %propagate.1 = bf16[16,128,256]{2,1,0:T(8,128)(2,1)S(1)} custom-call(bf16[16,128,256]{2,1,0:T(8,128)(2,1)} %bitcast.3, bf16[256,128,128]{2,1,0:T(8,128)(2,1)} %tiles_hbm.1, s32[256]{0:T(256)} %cols_hbm.1, s32[1,4,4]{2,1,0:T(4,128)} %halo_hbm.1), custom_call_target="tpu_custom_call" | custom-call | tf_op jit(solution)/shard_map/propagate/pallas_call | solution.py:262
  56.8 1.0 %copy.6 = bf16[2048,256]{1,0:T(8,128)(2,1)} copy(bf16[2048,256]{1,0:T(8,128)(2,1)S(1)} %bitcast.2) | data formatting | bytes 2097152

commit v4 on v3

--- a/solution.py
+++ b/solution.py
@@ -17,7 +17,7 @@
 
 def kernel(
     feat_hbm, tiles_hbm, cols_hbm, halo_hbm, out,
-    cols, halo, fbuf, tiles, tab0, tab1, tab2, snd0, snd1, snd2, u1, u2, u3,
+    cols, halo, fbuf, tiles, tab0, tab1, tab2, snd0, snd1, snd2, u1, u2, last,
     gram, early1, early2, late1, late2,
     load_sem, halo_send, halo_recv, ar_send, ar_recv,
 ):
@@ -42,7 +42,7 @@
         d = lax.rem(me + shift + shards, shards)
         return (d // nrep, d % nrep)
 
-    leading, across, trailing, staying = 1 - core, 3 - core, core, 2 + core
+    leading, trailing, across, staying = 1 - core, core, 3 - core, 2 + core
 
     loads = [
         pltpu.make_async_copy(feat_hbm, fbuf, load_sem.at[0]),
@@ -96,7 +96,7 @@
         for o in range(PEERS):
             snd0[o * SLOTS + j] = fbuf[halo[0, o, j]]
     pl.semaphore_wait(barrier, PEERS + 30)
-    for o in (leading, across, trailing, staying):
+    for o in (leading, trailing, across, staying):
         for j in range(SLOTS):
             halo_copy(0, o, j).start()
     for i in (1, 2, 3):
@@ -119,23 +119,43 @@
                 return 0
             lax.fori_loop(0, SLOTS, body, 0)
 
-        for o in (leading, across, trailing, staying):
+        for o in (leading, trailing, across, staying):
             one(o)
 
-    def own_pass(step, keep, others, first):
+    def each_block(work):
         def body(q, _):
             for part in range(4):
-                r = q * 4 + part
-                u = row_block(tab[step - 1], r)
-                keep[r] = u
-                if step < ITERS:
-                    tab[step][r] = u.astype(jnp.bfloat16)
-                for i, other in enumerate(others):
-                    gram[first + i] += fold(other[r].astype(jnp.float32) * u)
-                gram[first + len(others)] += fold(u * u)
+                work(q * 4 + part)
             return 0
 
-        lax.fori_loop(0, 4, body, 0)
+        lax.fori_loop(0, NB // 4, body, 0)
+
+    def wide_f(r):
+        return fbuf[r].astype(jnp.float32)
+
+    def own_first(r):
+        u = row_block(tab0, r)
+        u1[r] = u
+        tab1[r] = u.astype(jnp.bfloat16)
+        f = wide_f(r)
+        gram[0] += fold(f * f)
+        gram[1] += fold(f * u)
+        gram[2] += fold(u * u)
+
+    def own_second(r):
+        u = row_block(tab1, r)
+        u2[r] = u
+        tab2[r] = u.astype(jnp.bfloat16)
+        w = KEEP * u + TELEPORT * u1[r]
+        gram[3] += fold(w * w)
+        gram[4] += fold(w * wide_f(r))
+
+    def own_third(r):
+        w = KEEP * row_block(tab2, r) + TELEPORT * u2[r]
+        last[r] = w
+        gram[5] += fold(w * w)
+        gram[6] += fold(w * u1[r])
+        gram[7] += fold(w * wide_f(r))
 
     def pack(buf, mine, first, count):
         for i in range(count):
@@ -164,23 +184,17 @@
 
     wait_halo(0)
     send_pass(1)
-    def ff_body(r, _):
-        f = fbuf[r].astype(jnp.float32)
-        gram[0] += fold(f * f)
-        return 0
-    lax.fori_loop(0, NB, ff_body, 0)
-    own_pass(1, u1, (fbuf,), 1)
+    each_block(own_first)
     wait_halo(1)
     send_pass(2)
-    own_pass(2, u2, (fbuf, u1), 3)
-    early1[plane, pl.ds(12, 4), :] = jnp.zeros((4, HALF), jnp.float32)
-    pack(early1, plane, 0, 6)
+    each_block(own_second)
+    pack(early1, plane, 0, 5)
     early_a = stage(0, early1, plane, plane_member)
     for copy in early_a:
         copy.start()
     wait_halo(2)
-    own_pass(3, u3, (fbuf, u1, u2), 6)
-    pack(late1, plane, 6, 4)
+    each_block(own_third)
+    pack(late1, plane, 5, 3)
     late_a = stage(2, late1, plane, plane_member)
     for copy in late_a:
         copy.start()
@@ -190,52 +204,45 @@
     early_b = stage(1, early2, column, column_member)
     for copy in early_b:
         copy.start()
-    for copy in early_b:
-        copy.wait_recv()
-    early = total_of(early2)
-
-    def row(block, i):
-        return jnp.concatenate([block[2 * i:2 * i + 1], block[2 * i + 1:2 * i + 2]], axis=1)
-
-    def scale_of(mass):
-        return 1.0 / jnp.sqrt(0.05 + mass / vertices)
-
-    a, b = KEEP, TELEPORT
-    ff, f1, g11, f2, g12, g22 = (row(early, i) for i in range(6))
-    s1 = scale_of(a * a * g11 + 2 * a * b * f1 + b * b * ff)
-    w22 = a * a * g22 + 2 * a * b * g12 + b * b * g11
-    w2f = a * f2 + b * f1
-    s2 = scale_of((a * s1) * (a * s1) * w22 + 2 * a * b * s1 * w2f + b * b * ff)
-    c3 = a * a * a * s1 * s2
-    c2 = a * a * b * s1 * s2
-    c1 = a * b * s2
-
     for copy in late_a:
         copy.wait_recv()
-    part = total_of(late1)
-    f3, g13, g23, g33 = (row(part, i) for i in range(4))
-    part = c3 * c3 * g33 + 2 * c3 * (c2 * g23 + c1 * g13 + b * f3)
-    for h in range(2):
-        late2[column, pl.ds(h, 1), :] = part[:, h * HALF:(h + 1) * HALF]
+    late2[column] = total_of(late1)
     late_b = stage(3, late2, column, column_member)
     for copy in late_b:
         copy.start()
-    known = (
-        c2 * c2 * g22 + c1 * c1 * g11 + b * b * ff
-        + 2 * c2 * (c1 * g12 + b * f2) + 2 * b * c1 * f1
-    )
+    for copy in early_b:
+        copy.wait_recv()
+
+    def row(block, i):
+        return jnp.concatenate([block[2 * i:2 * i + 1], block[2 * i + 1:2 * i + 2]], axis=1)
+
+    def scale_of(mass):
+        return 1.0 / jnp.sqrt(0.05 + mass / vertices)
+
+    a, b = KEEP, TELEPORT
+    early = total_of(early2)
+    ff, f1, g11, ww2, wf2 = (row(early, i) for i in range(5))
+    s1 = scale_of(a * a * g11 + 2 * a * b * f1 + b * b * ff)
+    c = a * s1
+    s2 = scale_of(c * c * ww2 + 2 * b * c * wf2 + b * b * ff)
+    c3 = a * a * s1 * s2
+    c1 = a * b * s2
 
     def blend(r, _):
-        u3[r] = c3 * u3[r] + c2 * u2[r] + c1 * u1[r] + b * fbuf[r].astype(jnp.float32)
+        last[r] = c3 * last[r] + c1 * u1[r] + b * wide_f(r)
         return 0
 
     lax.fori_loop(0, NB, blend, 0)
     for copy in late_b:
         copy.wait_recv()
-    s3 = scale_of(known + row(total_of(late2), 0))
+    ww3, w13, wf3 = (row(total_of(late2), i) for i in range(3))
+    s3 = scale_of(
+        c3 * c3 * ww3 + c1 * c1 * g11 + b * b * ff
+        + 2 * c3 * (c1 * w13 + b * wf3) + 2 * b * c1 * f1
+    )
 
     def finish(r, _):
-        out[r] = (u3[r] * s3).astype(jnp.bfloat16)
+        out[r] = (last[r] * s3).astype(jnp.bfloat16)
         return 0
 
     lax.fori_loop(0, NB, finish, 0)
@@ -272,11 +279,11 @@
             table, table, table,
             blocks, blocks, blocks,
             wide, wide, wide,
-            pltpu.VMEM((10, 8, classes), jnp.float32),
-            pltpu.VMEM((16, 16, HALF), jnp.float32),
-            pltpu.VMEM((16, 16, HALF), jnp.float32),
-            pltpu.VMEM((16, 8, HALF), jnp.float32),
-            pltpu.VMEM((16, 2, HALF), jnp.float32),
+            pltpu.VMEM((8, 8, classes), jnp.float32),
+            pltpu.VMEM((16, 10, HALF), jnp.float32),
+            pltpu.VMEM((16, 10, HALF), jnp.float32),
+            pltpu.VMEM((16, 6, HALF), jnp.float32),
+            pltpu.VMEM((16, 6, HALF), jnp.float32),
             pltpu.SemaphoreType.DMA((5,)),
             pltpu.SemaphoreType.DMA((ITERS, NB)),
             pltpu.SemaphoreType.DMA((ITERS, NB)),

time: 57.9 us -> 54.3 us (0.938)
  Pallas kernels: 56.8 us -> 53.2 us
    pallas_call x1, Pallas kernels: 56.8 us -> 53.2 us  [local(): pl.pallas_call(kernel, out_shape=jax.ShapeDtypeStruct(rows, jnp.bfloat16)...]
where the time goes in v4:
time: 54.3 us; the launch traced here: 54.2 us
  Pallas kernels  53.2 us (98%)
  local copies, waits for them, and re-layouts  0.97 us (2%)
    pallas_call x1, Pallas kernels, local(): pl.pallas_call(kernel, out_shape=jax.ShapeDtypeStruct(rows, jnp.bfloat16)...  53.2 us

profile of v4, /device:TPU:1, one launch (start us, length us, event | category | flops | bytes accessed | tf_op | source)
XLA Modules:
  0.0 54.2 jit_solution(2844083581109157845)
XLA Ops:
  0.0 53.2 %propagate.1 = bf16[16,128,256]{2,1,0:T(8,128)(2,1)S(1)} custom-call(bf16[16,128,256]{2,1,0:T(8,128)(2,1)} %bitcast.3, bf16[256,128,128]{2,1,0:T(8,128)(2,1)} %tiles_hbm.1, s32[256]{0:T(256)} %cols_hbm.1, s32[1,4,4]{2,1,0:T(4,128)} %halo_hbm.1), custom_call_target="tpu_custom_call" | custom-call | tf_op jit(solution)/shard_map/propagate/pallas_call | solution.py:269
  53.2 1.0 %copy.6 = bf16[2048,256]{1,0:T(8,128)(2,1)} copy(bf16[2048,256]{1,0:T(8,128)(2,1)S(1)} %bitcast.2) | data formatting | bytes 2097152

commit v5 on v4

--- a/solution.py
+++ b/solution.py
@@ -17,7 +17,8 @@
 
 def kernel(
     feat_hbm, tiles_hbm, cols_hbm, halo_hbm, out,
-    cols, halo, fbuf, tiles, tab0, tab1, tab2, snd0, snd1, snd2, u1, u2, last,
+    cols, halo, fbuf, tiles, tab0a, tab0b, tab1a, tab1b, tab2a, tab2b,
+    snd0a, snd0b, snd1a, snd1b, snd2a, snd2b, u1, u2, last,
     gram, early1, early2, late1, late2,
     load_sem, halo_send, halo_recv, ar_send, ar_recv,
 ):
@@ -44,15 +45,17 @@
 
     leading, trailing, across, staying = 1 - core, core, 3 - core, 2 + core
 
+    low, high = pl.ds(0, HALF), pl.ds(HALF, HALF)
     loads = [
-        pltpu.make_async_copy(feat_hbm, fbuf, load_sem.at[0]),
-        pltpu.make_async_copy(feat_hbm, tab0.at[pl.ds(0, NB)], load_sem.at[1]),
-        pltpu.make_async_copy(tiles_hbm, tiles, load_sem.at[2]),
-        pltpu.make_async_copy(cols_hbm, cols, load_sem.at[3]),
-        pltpu.make_async_copy(halo_hbm, halo, load_sem.at[4]),
+        pltpu.make_async_copy(halo_hbm, halo, load_sem.at[0]),
+        pltpu.make_async_copy(feat_hbm, fbuf, load_sem.at[1]),
+        pltpu.make_async_copy(cols_hbm, cols, load_sem.at[2]),
+        pltpu.make_async_copy(feat_hbm.at[:, :, low], tab0a.at[pl.ds(0, NB)], load_sem.at[3]),
+        pltpu.make_async_copy(feat_hbm.at[:, :, high], tab0b.at[pl.ds(0, NB)], load_sem.at[4]),
+        pltpu.make_async_copy(tiles_hbm, tiles, load_sem.at[5]),
     ]
-    for i in (4, 0, 3, 1, 2):
-        loads[i].start()
+    for copy in loads:
+        copy.start()
 
     barrier = pltpu.get_barrier_semaphore()
     for o in range(PEERS):
@@ -64,25 +67,26 @@
             barrier, inc=1, device_id=column_member((column + k) % 16), device_id_type=MESH)
     gram[...] = jnp.zeros_like(gram)
 
-    snd, tab = (snd0, snd1, snd2), (tab0, tab1, tab2)
-
-    def halo_copy(step, o, j):
-        i = o * SLOTS + j
+    snd = ((snd0a, snd0b), (snd1a, snd1b), (snd2a, snd2b))
+    tab = ((tab0a, tab0b), (tab1a, tab1b), (tab2a, tab2b))
+
+    def halo_copy(step, half, o):
         return pltpu.make_async_remote_copy(
-            src_ref=snd[step].at[i],
-            dst_ref=tab[step].at[NB + i],
-            send_sem=halo_send.at[step, i],
-            recv_sem=halo_recv.at[step, i],
+            src_ref=snd[step][half].at[pl.ds(o * SLOTS, SLOTS)],
+            dst_ref=tab[step][half].at[pl.ds(NB + o * SLOTS, SLOTS)],
+            send_sem=halo_send.at[step * 2 + half, o],
+            recv_sem=halo_recv.at[step * 2 + half, o],
             device_id=peer(o),
             device_id_type=MESH,
         )
 
-    def row_block(table, r):
+    def row_block(halves, r):
         total = None
         for p in range(NB // 2):
-            t = r * NB + 2 * p
-            lhs = jnp.concatenate([tiles[t], tiles[t + 1]], axis=1)
-            rhs = jnp.concatenate([table[cols[t]], table[cols[t + 1]]], axis=0)
+            pair = (r * NB + 2 * p, r * NB + 2 * p + 1)
+            lhs = jnp.concatenate([tiles[t] for t in pair], axis=1)
+            rhs = jnp.concatenate(
+                [jnp.concatenate([h[cols[t]] for h in halves], axis=1) for t in pair], axis=0)
             term = jnp.dot(lhs, rhs, preferred_element_type=jnp.float32)
             total = term if total is None else total + term
         return total
@@ -90,37 +94,34 @@
     def fold(x):
         return jnp.sum(x.reshape(NB, 8, x.shape[-1]), axis=0)
 
-    loads[4].wait()
     loads[0].wait()
-    for j in range(SLOTS):
+    loads[1].wait()
+    for o in range(PEERS):
+        for j in range(SLOTS):
+            block = fbuf[halo[0, o, j]]
+            snd0a[o * SLOTS + j] = block[:, :HALF]
+            snd0b[o * SLOTS + j] = block[:, HALF:]
+    pl.semaphore_wait(barrier, PEERS + 30)
+    for half in range(2):
+        for o in (leading, trailing, across, staying):
+            halo_copy(0, half, o).start()
+    for copy in loads[2:]:
+        copy.wait()
+
+    def wait_halo(step, half):
         for o in range(PEERS):
-            snd0[o * SLOTS + j] = fbuf[halo[0, o, j]]
-    pl.semaphore_wait(barrier, PEERS + 30)
-    for o in (leading, trailing, across, staying):
-        for j in range(SLOTS):
-            halo_copy(0, o, j).start()
-    for i in (1, 2, 3):
-        loads[i].wait()
-
-    def wait_halo(step):
-        for o in range(PEERS):
+            halo_copy(step, half, o).wait_recv()
+
+    def send_pass(step, half):
+        def body(g, _):
+            o = g // 2 * 2 + (1 - core) + g % 2 * (2 * core - 1)
             for j in range(SLOTS):
-                halo_copy(step, o, j).wait_recv()
-
-    def send_pass(step):
-        def send(o, j):
-            i = o * SLOTS + j
-            snd[step][i] = row_block(tab[step - 1], halo[0, o, j]).astype(jnp.bfloat16)
-            halo_copy(step, o, j).start()
-
-        def one(o):
-            def body(j, _):
-                send(o, j)
-                return 0
-            lax.fori_loop(0, SLOTS, body, 0)
-
-        for o in (leading, trailing, across, staying):
-            one(o)
+                u = row_block((tab[step - 1][half],), halo[0, o, j])
+                snd[step][half][o * SLOTS + j] = u.astype(jnp.bfloat16)
+            halo_copy(step, half, o).start()
+            return 0
+
+        lax.fori_loop(0, PEERS, body, 0)
 
     def each_block(work):
         def body(q, _):
@@ -134,24 +135,26 @@
         return fbuf[r].astype(jnp.float32)
 
     def own_first(r):
-        u = row_block(tab0, r)
+        u = row_block(tab[0], r)
         u1[r] = u
-        tab1[r] = u.astype(jnp.bfloat16)
+        tab1a[r] = u[:, :HALF].astype(jnp.bfloat16)
+        tab1b[r] = u[:, HALF:].astype(jnp.bfloat16)
         f = wide_f(r)
         gram[0] += fold(f * f)
         gram[1] += fold(f * u)
         gram[2] += fold(u * u)
 
     def own_second(r):
-        u = row_block(tab1, r)
+        u = row_block(tab[1], r)
         u2[r] = u
-        tab2[r] = u.astype(jnp.bfloat16)
+        tab2a[r] = u[:, :HALF].astype(jnp.bfloat16)
+        tab2b[r] = u[:, HALF:].astype(jnp.bfloat16)
         w = KEEP * u + TELEPORT * u1[r]
         gram[3] += fold(w * w)
         gram[4] += fold(w * wide_f(r))
 
     def own_third(r):
-        w = KEEP * row_block(tab2, r) + TELEPORT * u2[r]
+        w = KEEP * row_block(tab[2], r) + TELEPORT * u2[r]
         last[r] = w
         gram[5] += fold(w * w)
         gram[6] += fold(w * u1[r])
@@ -182,17 +185,20 @@
             total = total + buf[i]
         return total
 
-    wait_halo(0)
-    send_pass(1)
+    for half in range(2):
+        wait_halo(0, half)
+        send_pass(1, half)
     each_block(own_first)
-    wait_halo(1)
-    send_pass(2)
+    for half in range(2):
+        wait_halo(1, half)
+        send_pass(2, half)
     each_block(own_second)
     pack(early1, plane, 0, 5)
     early_a = stage(0, early1, plane, plane_member)
     for copy in early_a:
         copy.start()
-    wait_halo(2)
+    wait_halo(2, 0)
+    wait_halo(2, 1)
     each_block(own_third)
     pack(late1, plane, 5, 3)
     late_a = stage(2, late1, plane, plane_member)
@@ -248,9 +254,9 @@
     lax.fori_loop(0, NB, finish, 0)
 
     for step in range(ITERS):
-        for j in range(SLOTS):
+        for half in range(2):
             for o in range(PEERS):
-                halo_copy(step, o, j).wait_send()
+                halo_copy(step, half, o).wait_send()
     for copy in early_a + early_b + late_a + late_b:
         copy.wait_send()
 
@@ -259,7 +265,8 @@
     classes = features.shape[1]
     rows = (NB, TILE, classes)
     anywhere = pl.BlockSpec(memory_space=pltpu.HBM)
-    table = pltpu.VMEM((2 * NB, TILE, classes), jnp.bfloat16)
+    table = pltpu.VMEM((2 * NB, TILE, HALF), jnp.bfloat16)
+    parcels = pltpu.VMEM((NB, TILE, HALF), jnp.bfloat16)
     blocks = pltpu.VMEM(rows, jnp.bfloat16)
     wide = pltpu.VMEM(rows, jnp.float32)
     inputs = [
@@ -276,17 +283,17 @@
             pltpu.SMEM(halo_rows.shape, jnp.int32),
             blocks,
             pltpu.VMEM(tile_values.shape, jnp.bfloat16),
-            table, table, table,
-            blocks, blocks, blocks,
+            *[table] * 6,
+            *[parcels] * 6,
             wide, wide, wide,
             pltpu.VMEM((8, 8, classes), jnp.float32),
             pltpu.VMEM((16, 10, HALF), jnp.float32),
             pltpu.VMEM((16, 10, HALF), jnp.float32),
             pltpu.VMEM((16, 6, HALF), jnp.float32),
             pltpu.VMEM((16, 6, HALF), jnp.float32),
-            pltpu.SemaphoreType.DMA((5,)),
-            pltpu.SemaphoreType.DMA((ITERS, NB)),
-            pltpu.SemaphoreType.DMA((ITERS, NB)),
+            pltpu.SemaphoreType.DMA((6,)),
+            pltpu.SemaphoreType.DMA((2 * ITERS, PEERS)),
+            pltpu.SemaphoreType.DMA((2 * ITERS, PEERS)),
             pltpu.SemaphoreType.DMA((4, 15)),
             pltpu.SemaphoreType.DMA((4, 15)),
         ],

time: 54.3 us -> 50.3 us (0.926)
  Pallas kernels: 53.2 us -> 49.2 us
    pallas_call x1, Pallas kernels: 53.2 us -> 49.2 us  [local(): pl.pallas_call(kernel, out_shape=jax.ShapeDtypeStruct(rows, jnp.bfloat16)...]
where the time goes in v5:
time: 50.3 us; the launch traced here: 50.2 us
  Pallas kernels  49.2 us (98%)
  local copies, waits for them, and re-layouts  0.97 us (2%)
    pallas_call x1, Pallas kernels, local(): pl.pallas_call(kernel, out_shape=jax.ShapeDtypeStruct(rows, jnp.bfloat16)...  49.2 us

profile of v5, /device:TPU:1, one launch (start us, length us, event | category | flops | bytes accessed | tf_op | source)
XLA Modules:
  0.0 50.2 jit_solution(1482652235990573241)
XLA Ops:
  0.0 49.2 %propagate.1 = bf16[16,128,256]{2,1,0:T(8,128)(2,1)S(1)} custom-call(bf16[16,128,256]{2,1,0:T(8,128)(2,1)} %bitcast.3, bf16[256,128,128]{2,1,0:T(8,128)(2,1)} %tiles_hbm.1, s32[256]{0:T(256)} %cols_hbm.1, s32[1,4,4]{2,1,0:T(4,128)} %halo_hbm.1), custom_call_target="tpu_custom_call" | custom-call | tf_op jit(solution)/shard_map/propagate/pallas_call | solution.py:276
  49.2 1.0 %copy.6 = bf16[2048,256]{1,0:T(8,128)(2,1)} copy(bf16[2048,256]{1,0:T(8,128)(2,1)S(1)} %bitcast.2) | data formatting | bytes 2097152
